TPU v7x, 32 devices: a whole 2x2x4 slice. The times are simulated.
32 devices in a mesh: seq: 16 (over z, y, x), head: 2 (over core).
Axes of the slice: x: 2, y: 2, z: 4, core: 2. Of those that a mesh axis runs over, the one named last changes fastest.
Arguments:
- queries: bfloat16 [2048, 2048], P('seq', 'head'), may hold values from -6 to 6
- keys: bfloat16 [2048, 512], P('seq', 'head'), may hold values from -6 to 6
- values: bfloat16 [2048, 512], P('seq', 'head'), may hold values from -6 to 6
- tile_mask: int32 [32, 32], replicated, may hold values from 0 to 1, as said below
- out_weight: bfloat16 [2048, 4096], P('head'), may hold values from -0.5 to 0.5
Outputs:
- mixed: bfloat16 [2048, 4096], P(('seq', 'head'))
Inputs may be any that keep to these rules, and one draw needn't show every extreme that they name: tile_mask[i, j] is 1 for i == j, 0 for j > i, and 0 or 1 below the diagonal.
All inputs are finite; a program needn't handle non-finite values.
Results may differ from a plain program's by a relative error of at most 0.01.
Values may be sent and summed in bfloat16 or wider, within the bound.
A program may use at most 128 MiB of HBM per device.

v0:
```python
import math

import jax
import jax.numpy as jnp
from jax import lax
from jax.sharding import PartitionSpec as P

HD = 128
TILE = 64


MASK_FLOOR = -1e30


def per_device(queries, keys, values, tile_mask, out_weight):
    row_count = queries.shape[0]
    local_groups = keys.shape[1] // HD
    group = queries.shape[1] // HD // local_groups
    scale = 1.0 / math.sqrt(HD)
    seq_place = lax.axis_index("seq")
    query_index = seq_place * row_count + jnp.arange(row_count, dtype=jnp.int32)
    query_block = queries.reshape(row_count, local_groups, group, HD)
    query_tiles = query_index[::TILE] // TILE
    mask_rows = jnp.take(tile_mask, query_tiles, axis=0)

    def block_step(state, key_part, value_part, key_start):
        width = key_part.shape[0]
        key_index = key_start + jnp.arange(width, dtype=jnp.int32)
        tile_open = jnp.repeat(jnp.take(mask_rows, key_index // TILE, axis=1) > 0, TILE, axis=0)
        allowed = tile_open & (key_index[None, :] <= query_index[:, None])
        best, total, running = state
        allowed_wide = allowed[:, None, None, :]
        scores = (
            jnp.einsum(
                "qgrd,kgd->qgrk",
                query_block,
                key_part.reshape(width, local_groups, HD),
                preferred_element_type=jnp.float32,
            )
            * scale
        )
        masked = jnp.where(allowed_wide, scores, MASK_FLOOR)
        new_best = jnp.maximum(best, jnp.max(masked, axis=-1))
        weights = jnp.where(allowed_wide, jnp.exp(masked - new_best[..., None]), 0.0)
        rescale = jnp.exp(best - new_best)
        total = total * rescale + jnp.sum(weights, axis=-1)
        product = jnp.einsum(
            "qgrk,kgd->qgrd",
            weights.astype(jnp.bfloat16),
            value_part.reshape(width, local_groups, HD),
            preferred_element_type=jnp.float32,
        )
        running = running * rescale[..., None] + product
        return (new_best, total, running)

    initial = (
        jnp.full((row_count, local_groups, group), MASK_FLOOR, jnp.float32),
        jnp.zeros((row_count, local_groups, group), jnp.float32),
        jnp.zeros((row_count, local_groups, group, HD), jnp.float32),
    )
    carry = initial
    key_piece = lax.all_gather(keys, "seq", axis=0, tiled=True)
    value_piece = lax.all_gather(values, "seq", axis=0, tiled=True)
    width = key_piece.shape[0]
    block_size = math.gcd(width, 2048)
    count = width // block_size
    key_blocks = key_piece.reshape(count, block_size, key_piece.shape[1])
    value_blocks = value_piece.reshape(count, block_size, value_piece.shape[1])
    offsets = block_size * jnp.arange(count, dtype=jnp.int32)

    def advance(state, item):
        key_part, value_part, key_start = item
        return (block_step(state, key_part, value_part, key_start), None)

    carry, unused = lax.scan(advance, carry, (key_blocks, value_blocks, offsets))
    best, total, running = carry
    attended = (
        (running / total[..., None])
        .reshape(row_count, local_groups * group * HD)
        .astype(jnp.bfloat16)
    )
    return lax.psum_scatter(
        jnp.dot(attended, out_weight, preferred_element_type=jnp.float32).astype(jnp.bfloat16),
        "head",
        scatter_dimension=0,
        tiled=True,
    )


def solution(mesh):
    placed = (P("seq", "head"), P("seq", "head"), P("seq", "head"), P(), P("head", None))
    return jax.shard_map(
        per_device, mesh=mesh, in_specs=placed, out_specs=P(("seq", "head"), None), check_vma=False
    )
```

profile of v0, /device:TPU:25, one launch (start us, length us, event | category | flops | bytes accessed | tf_op | source)
XLA Modules:
  0.0 146.6 jit_solution(15410946941550882141)
XLA Ops:
  6.5 1.6 %copy.13 = bf16[128,256]{0,1:T(8,128)(2,1)} copy(bf16[128,256]{1,0:T(8,128)(2,1)} %param.6) | data formatting | bytes 131072 | tf_op args[1]
  8.1 0.0 all-gather.5.cloned.1.call-start
  8.2 0.7 all-gather.5.cloned.1.call-update
  8.9 0.0 reduce-scatter.2.cloned.1.call-start
  9.0 0.1 slice.3
  9.1 0.6 gather_fusion
  9.7 0.1 broadcast_select_fusion
  9.8 0.1 copy.10
  9.9 5.5 %gather_fusion.1 = s32[2048,2]{1,0:T(8,128)S(1)} fusion(s32[2,32]{0,1:T(8,128)S(1)} %copy.10, s32[2048]{0:T(1024)S(1)} %broadcast_clamp_fusion), kind=kCustom, calls=%fused_computation.1 | custom fusion | bytes 40960 | tf_op jit(solution)/shard_map/while/body/eval_jaxpr/jit(_take)/gather | solution.py:29
  15.3 0.3 fusion.13
  15.7 0.4 copy.11
  16.0 0.3 fusion.12
  16.3 0.4 copy.12
  16.7 1.1 reshape.123
  17.9 41.0 %all-gather.3.cloned.1.call-done = bf16[2048,256]{0,1:T(8,128)(2,1)} async-done(((bf16[128,256]{0,1:T(8,128)(2,1)}), bf16[2048,256]{0,1:T(8,128)(2,1)}) %all-gather.3.cloned.1.call-update) | async-done | bytes 1048592 | tf_op jit(solution)/shard_map/all_gather | solution.py:62
  58.8 2.7 %fusion = (f32[128,2,4]{0,2,1:T(4,128)S(1)}, f32[2,2048,128,4]{2,1,3,0:T(8,128)S(1)}) fusion(pred[128,2048]{0,1:T(8,128)(4,1)S(1)} %copy.12, bf16[2048,2,128,1]{0,2,3,1:T(8,128)(2,1)} %bitcast.47, bf16[128,2,4,128]{3,2,1,0:T(4,128)(2,1)S(1)} %reshape.123), kind=kOutput, calls=%fused_computation.4 | convolution fusion | flops 543161344 | bytes 9965568 | tf_op jit(solution)/shard_map/while/body/eval_jaxpr/qgrd,kgd->qgrk/dot_general | solution.py:34
  61.6 3.2 %copy-done.1 = f32[2,2048,128,4]{2,1,3,0:T(8,128)} copy-done((f32[2,2048,128,4]{2,1,3,0:T(8,128)}, f32[2,2048,128,4]{2,1,3,0:T(8,128)S(1)}, u32[]{:S(2)}) %copy-start.1) | copy-done | bytes 8388632
  64.8 2.0 %fusion.1 = f32[128,2,4]{0,2,1:T(4,128)S(1)} fusion(f32[2,2048,128,4]{2,1,3,0:T(8,128)S(1)} %get-tuple-element.26, f32[128,2,4]{0,2,1:T(4,128)S(1)} %broadcast_maximum_fusion, pred[128,2048]{0,1:T(8,128)(4,1)S(1)} %copy.12), kind=kLoop, calls=%fused_computation.5 | loop fusion | flops 10484736 | bytes 8658944 | tf_op jit(solution)/shard_map/while/body/eval_jaxpr/reduce_sum | solution.py:46
  66.8 49.1 %all-gather.5.cloned.1.call-done = bf16[2048,256]{1,0:T(8,128)(2,1)} async-done(((bf16[128,256]{1,0:T(8,128)(2,1)}), bf16[2048,256]{1,0:T(8,128)(2,1)}) %all-gather.5.cloned.1.call-update) | async-done | bytes 1048592 | tf_op jit(solution)/shard_map/all_gather | solution.py:63
  115.9 1.5 %copy.16 = bf16[2048,256]{0,1:T(8,128)(2,1)S(1)} copy(bf16[2048,256]{1,0:T(8,128)(2,1)} %all-gather.5.cloned.1.call-done) | data formatting | bytes 2097152 | tf_op jit(solution)/shard_map/all_gather | solution.py:63
  117.4 5.5 %fusion.17 = bf16[128,2,4,128]{0,3,2,1:T(8,128)(2,1)S(1)} fusion(bf16[2048,2,128,1]{0,2,3,1:T(8,128)(2,1)S(1)} %bitcast.48, f32[2,2048,128,4]{2,1,3,0:T(8,128)} %copy-done.1, f32[128,2,4]{0,2,1:T(4,128)S(1)} %broadcast_maximum_fusion, pred[128,2048]{0,1:T(8,128)(4,1)S(1)} %copy.12, f32[128,2,4]{0,2,1:T(4,128)S(1)} %get-tuple-element.24, ...), kind=kOutput, calls=%fused_computation.17 | convolution fusion | flops 547749888 | bytes 9973760 | tf_op jit(solution)/shard_map/while/body/eval_jaxpr/qgrk,kgd->qgrd/dot_general | solution.py:47
  122.9 5.6 %convolution_convert_fusion = bf16[128,4096]{1,0:T(8,128)(2,1)} fusion(bf16[128,1024]{0,1:T(8,128)(2,1)S(1)} %bitcast.49, bf16[1024,4096]{1,0:T(8,128)(2,1)} %param.9), kind=kOutput, calls=%fused_computation.7 | convolution fusion | flops 1074266112 | bytes 9699328 | tf_op jit(solution)/shard_map/dot_general | solution.py:83
  128.6 0.0 reduce-scatter.2.cloned.1.call-update
  128.6 11.5 %reduce-scatter.2.cloned.1.call-done = bf16[64,4096]{1,0:T(8,128)(2,1)} async-done(((bf16[128,4096]{1,0:T(8,128)(2,1)}), bf16[64,4096]{1,0:T(8,128)(2,1)}) %reduce-scatter.2.cloned.1.call-update) | async-done | bytes 524304 | tf_op jit(solution)/shard_map/reduce_scatter | solution.py:82
  (13 shorter events, 0.1 us)
Async XLA Ops:
  6.5 2.6 %copy-start = (s32[32,32]{1,0:T(8,128)S(1)}, s32[32,32]{1,0:T(8,128)}, u32[]{:S(2)}) copy-start(s32[32,32]{1,0:T(8,128)} %param.8) | copy-start | bytes 12292
  6.5 52.3 %all-gather.3.cloned.1.call-start = ((), (), s32[]{:S(2)}) async-start(), calls=%async_computation.1 | async-start | bytes 1114112 | tf_op jit(solution)/shard_map/all_gather | solution.py:62
  8.1 107.8 %all-gather.5.cloned.1.call-start = ((), (), s32[]{:S(2)}) async-start(), calls=%async_computation.2 | async-start | bytes 1114112 | tf_op jit(solution)/shard_map/all_gather | solution.py:63
  8.9 131.2 %reduce-scatter.2.cloned.1.call-start = ((), (), s32[]{:S(2)}) async-start(), calls=%async_computation.3 | async-start | bytes 1572864 | tf_op jit(solution)/shard_map/reduce_scatter | solution.py:82
  61.6 3.2 %copy-start.1 = (f32[2,2048,128,4]{2,1,3,0:T(8,128)}, f32[2,2048,128,4]{2,1,3,0:T(8,128)S(1)}, u32[]{:S(2)}) copy-start(f32[2,2048,128,4]{2,1,3,0:T(8,128)S(1)} %get-tuple-element.26) | copy-start | bytes 25165828
Sparse Core Ops, SparseCore 0:
  10.0 48.7 all-gather.2
  61.6 54.2 all-gather.4
  128.7 11.3 reduce-scatter.1
where the time goes:
time: 148 us; the launch traced here: 147 us
  waiting for transfers between devices  102 us (69%)
  local copies, waits for them, and re-layouts  14.4 us (10%)
  matrix products  13.9 us (9%)
  between operations  13.2 us (9%)
  other arithmetic  2.74 us (2%)
    all_gather x1, waiting for transfers between devices, per_device(): value_piece = lax.all_gather(values, 'seq', axis=0, tiled=True)  49.1 us
    all_gather x1, waiting for transfers between devices, per_device(): key_piece = lax.all_gather(keys, 'seq', axis=0, tiled=True)  41 us
    reduce_scatter x1, waiting for transfers between devices, per_device(): lax.psum_scatter(jnp.dot(attended, out_weight, preferred_element_type=jnp...  11.5 us
    dot_general x1, matrix products, per_device(): jnp.dot(attended, out_weight, preferred_element_type=jnp.float32)  5.64 us
    dot_general x1, matrix products, block_step(): jnp.einsum('qgrk,kgd->qgrd', weights.astype(jnp.bfloat16), value_part.res...  5.52 us
    gather x1, local copies, waits for them, and re-layouts, block_step(): jnp.take(mask_rows, key_index // TILE, axis=1) > 0  5.46 us
    unnamed x5, local copies, waits for them, and re-layouts  4.8 us
  transfers between devices with their start and end apart: 3, of which 3 were waited for; matrix products, arithmetic and copies ran while one was open for 9% of the time, Pallas kernels for 0%

commit v1 on v0

v1 whole, which is shorter than its diff:
```python
import functools
import math

import jax
import jax.numpy as jnp
from jax import lax
from jax.experimental import pallas as pl
from jax.experimental.pallas import tpu as pltpu
from jax.sharding import PartitionSpec as P

HD = 128
MASK_FLOOR = -1e30
MESH = pl.DeviceIdType.MESH


def fused_kernel(
    dims,
    q_hbm, k_hbm, v_hbm, mask_ref, w_hbm,
    out_ref,
    q_in, kv_in, qbuf, kvbuf, wbuf, rowmask, best, acc, attbuf, abuf, part, sendbuf, rbuf,
    load_sem, w_sem, kv_send, kv_recv, q_send, q_recv, fwd_send, fwd_recv,
    a_send, a_recv, p_send, p_recv,
):
    planes, members, cores, local_groups, rows, heads, tile, blocks, width = dims
    place = lax.axis_index("seq")
    core = lax.axis_index("head")
    plane = place // members
    member = lax.rem(place, members)
    partner = 1 - core
    home = member // local_groups
    chunk = members * rows
    hw = heads * HD

    loads = [
        pltpu.make_async_copy(k_hbm, kv_in.at[0], load_sem.at[0]),
        pltpu.make_async_copy(v_hbm, kv_in.at[1], load_sem.at[1]),
        pltpu.make_async_copy(q_hbm, q_in, load_sem.at[2]),
    ]
    for load in loads:
        load.start()

    barrier = pltpu.get_barrier_semaphore()

    def greet(seq_to, head_to):
        pl.semaphore_signal(barrier, inc=1, device_id=(seq_to, head_to), device_id_type=MESH)

    for shift in range(members * cores):
        if shift == 0:
            continue
        other = lax.rem(member * cores + core + shift, members * cores)
        greet(plane * members + other // cores, lax.rem(other, cores))

    def greet_above(up, none):
        for l in range(local_groups):
            for kind in range(2):
                greet(up * members + core * local_groups + l, kind)
        return none

    def greet_below(down, none):
        for s in range(members):
            greet(down * members + s, home)
        return none

    lax.fori_loop(plane + 1, planes, greet_above, 0)
    lax.fori_loop(0, plane, greet_below, 0)

    w_copy = pltpu.make_async_copy(w_hbm, wbuf, w_sem)

    tiles = mask_ref.shape[0]
    row_at = plane * chunk + lax.broadcasted_iota(jnp.int32, (chunk, tiles), 0)
    tile_at = lax.broadcasted_iota(jnp.int32, (chunk, tiles), 1) * tile
    pick = jnp.where((row_at >= tile_at) & (row_at < tile_at + tile), 1.0, 0.0).astype(jnp.bfloat16)
    open_tiles = jnp.where(mask_ref[...] > 0, 1.0, 0.0).astype(jnp.bfloat16)
    rowmask[...] = jnp.dot(pick, open_tiles, preferred_element_type=jnp.float32).astype(jnp.bfloat16)

    for load in loads:
        load.wait()
    pl.semaphore_wait(barrier, members * cores - 1 + (planes - 1) * members)

    def kv_copy(up, l, kind):
        return pltpu.make_async_remote_copy(
            src_ref=kv_in.at[kind, :, pl.ds(l * HD, HD)],
            dst_ref=kvbuf.at[kind, pl.ds(pl.multiple_of(place * rows, rows), rows), :],
            send_sem=kv_send.at[up, l, kind],
            recv_sem=kv_recv.at[place],
            device_id=(up * members + core * local_groups + l, kind),
            device_id_type=MESH,
        )

    def send_above(step, none):
        up = planes - 1 - step
        for l in range(local_groups):
            for kind in range(2):
                kv_copy(up, l, kind).start()
        return none

    lax.fori_loop(0, planes - 1 - plane, send_above, 0)

    def kv_is_own(l, kind):
        return (core * local_groups + l == member) & (core == kind)

    for l in range(local_groups):
        for kind in range(2):
            own = kv_is_own(l, kind)

            @pl.when(own)
            def _():
                pltpu.make_async_copy(
                    kv_in.at[kind, :, pl.ds(l * HD, HD)],
                    kvbuf.at[kind, pl.ds(pl.multiple_of(place * rows, rows), rows), :],
                    kv_recv.at[place],
                ).start()

            @pl.when(jnp.logical_not(own))
            def _():
                kv_copy(plane, l, kind).start()

    def q_copy(l, e):
        return pltpu.make_async_remote_copy(
            src_ref=q_in.at[:, pl.ds((l * cores + e) * hw, hw)],
            dst_ref=qbuf.at[member],
            send_sem=q_send.at[l, e],
            recv_sem=q_recv.at[member],
            device_id=(plane * members + core * local_groups + l, e),
            device_id_type=MESH,
        )

    for l in range(local_groups):
        for e in range(cores):
            own = kv_is_own(l, e)

            @pl.when(own)
            def _():
                pltpu.make_async_copy(
                    q_in.at[:, pl.ds((l * cores + e) * hw, hw)], qbuf.at[member], q_recv.at[member]
                ).start()

            @pl.when(jnp.logical_not(own))
            def _():
                q_copy(l, e).start()

    w_copy.start()

    def fwd_copy(kc):
        where = pl.ds(pl.multiple_of(kc * chunk, chunk), chunk)
        return pltpu.make_async_remote_copy(
            src_ref=kvbuf.at[core, where, :],
            dst_ref=kvbuf.at[core, where, :],
            send_sem=fwd_send.at[kc],
            recv_sem=fwd_recv.at[kc],
            device_id=(place, partner),
            device_id_type=MESH,
        )

    def arrive(kc):
        for s in range(members):
            block = kvbuf.at[core, pl.ds(pl.multiple_of((kc * members + s) * rows, rows), rows), :]
            pltpu.make_async_copy(block, block, kv_recv.at[kc * members + s]).wait()
        fwd_copy(kc).start()

    def fwd_arrived(kc):
        block = kvbuf.at[partner, pl.ds(pl.multiple_of(kc * chunk, chunk), chunk), :]
        pltpu.make_async_copy(block, block, fwd_recv.at[kc]).wait()

    unit = math.log2(math.e) / math.sqrt(HD)

    def attend(kc, s, first):
        keys_here = (s + 1) * rows if first else chunk
        base = pl.multiple_of(kc * chunk, chunk)
        key_at = base + lax.broadcasted_iota(jnp.int32, (tiles, keys_here), 1)
        tile_from = lax.broadcasted_iota(jnp.int32, (tiles, keys_here), 0) * tile
        spread = jnp.where((key_at >= tile_from) & (key_at < tile_from + tile), 1.0, 0.0)
        opened = jnp.dot(
            rowmask[pl.ds(s * rows, rows), :],
            spread.astype(jnp.bfloat16),
            preferred_element_type=jnp.float32,
        )
        if first:
            r = s * rows + lax.broadcasted_iota(jnp.int32, (rows, keys_here), 0)
            u = lax.broadcasted_iota(jnp.int32, (rows, keys_here), 1)
            opened = jnp.where(u <= r, opened, 0.0)
        visible = opened > 0.5
        k_part = kvbuf[0, pl.ds(base, keys_here), :]
        v_part = kvbuf[1, pl.ds(base, keys_here), :]
        v_wide = jnp.concatenate([v_part, jnp.ones_like(v_part)], axis=1)
        for h in range(heads):
            scores = lax.dot_general(
                qbuf[s, :, h * HD : (h + 1) * HD],
                k_part,
                (((1,), (1,)), ((), ())),
                preferred_element_type=jnp.float32,
            )
            scores = jnp.where(visible, scores * unit, MASK_FLOOR)
            top = jnp.max(scores, axis=1, keepdims=True)
            if not first:
                before = best[h, s]
                top = jnp.maximum(before, top)
            weights = jnp.exp2(scores - top).astype(jnp.bfloat16)
            product = jnp.dot(weights, v_wide, preferred_element_type=jnp.float32)
            if not first:
                product = acc[h, s] * jnp.exp2(before - top) + product
            best[h, s] = top
            acc[h, s] = product

    arrive(plane)
    for s in range(members):
        block = qbuf.at[s]
        pltpu.make_async_copy(block, block, q_recv.at[s]).wait()
    fwd_arrived(plane)
    for s in range(members):
        attend(plane, s, True)

    def below(step, none):
        kc = plane - 1 - step
        arrive(kc)
        fwd_arrived(kc)
        for s in range(members):
            attend(kc, s, False)
        return none

    lax.fori_loop(0, plane, below, 0)

    slot = lax.rem(member, local_groups) * cores + core

    def a_copy(s):
        return pltpu.make_async_remote_copy(
            src_ref=attbuf.at[s],
            dst_ref=abuf.at[slot],
            send_sem=a_send.at[s],
            recv_sem=a_recv.at[slot],
            device_id=(plane * members + s, home),
            device_id_type=MESH,
        )

    def a_is_own(s):
        return (member == s) & (core == home)

    for s in range(members):
        for h in range(heads):
            total = acc[h, s]
            attbuf[s, :, h * HD : (h + 1) * HD] = (total[:, :HD] / total[:, HD:]).astype(jnp.bfloat16)

        @pl.when(a_is_own(s))
        def _():
            pltpu.make_async_copy(attbuf.at[s], abuf.at[slot], a_recv.at[slot]).start()

        @pl.when(jnp.logical_not(a_is_own(s)))
        def _():
            a_copy(s).start()

    w_copy.wait()
    for j in range(local_groups * cores):
        block = abuf.at[j]
        pltpu.make_async_copy(block, block, a_recv.at[j]).wait()

    half = rows // cores
    attended = jnp.concatenate([abuf[j] for j in range(local_groups * cores)], axis=1)

    def p_copy(j):
        return pltpu.make_async_remote_copy(
            src_ref=sendbuf.at[j, pl.ds(pl.multiple_of(partner * half, half), half), :],
            dst_ref=rbuf.at[j],
            send_sem=p_send.at[j],
            recv_sem=p_recv.at[j],
            device_id=(place, partner),
            device_id_type=MESH,
        )

    for j in range(blocks):
        product = jnp.dot(
            attended, wbuf[:, j * width : (j + 1) * width], preferred_element_type=jnp.float32
        )
        sendbuf[j] = product.astype(jnp.bfloat16)
        p_copy(j).start()
        part[j] = product
    for j in range(blocks):
        p_copy(j).wait_recv()
        mine = part[j, pl.ds(pl.multiple_of(core * half, half), half), :]
        out_ref[:, j * width : (j + 1) * width] = (mine + rbuf[j].astype(jnp.float32)).astype(
            out_ref.dtype
        )

    for j in range(blocks):
        p_copy(j).wait_send()
    for s in range(members):

        @pl.when(jnp.logical_not(a_is_own(s)))
        def _():
            a_copy(s).wait_send()

    for l in range(local_groups):
        for e in range(cores):

            @pl.when(jnp.logical_not(kv_is_own(l, e)))
            def _():
                q_copy(l, e).wait_send()
                kv_copy(plane, l, e).wait_send()

    def drain_above(step, none):
        up = planes - 1 - step
        for l in range(local_groups):
            for kind in range(2):
                kv_copy(up, l, kind).wait_send()
        return none

    lax.fori_loop(0, planes - 1 - plane, drain_above, 0)

    def drain_fwd(kc, none):
        fwd_copy(kc).wait_send()
        return none

    lax.fori_loop(0, plane + 1, drain_fwd, 0)


def per_device(sizes, queries, keys, values, tile_mask, out_weight):
    seq_size, cores = sizes
    rows = queries.shape[0]
    local_groups = keys.shape[1] // HD
    group = queries.shape[1] // HD // local_groups
    members = local_groups * cores
    planes = seq_size // members
    heads = group // cores
    tile = rows * seq_size // tile_mask.shape[0]
    columns = out_weight.shape[1]
    width = math.gcd(columns, 512)
    blocks = columns // width
    dims = (planes, members, cores, local_groups, rows, heads, tile, blocks, width)
    bf16, f32 = jnp.bfloat16, jnp.float32
    DMA = pltpu.SemaphoreType.DMA
    any_spec = pl.BlockSpec(memory_space=pl.ANY)
    vmem_spec = pl.BlockSpec(memory_space=pltpu.VMEM)
    return pl.pallas_call(
        functools.partial(fused_kernel, dims),
        out_shape=jax.ShapeDtypeStruct((rows // cores, columns), bf16),
        in_specs=[any_spec, any_spec, any_spec, vmem_spec, any_spec],
        out_specs=vmem_spec,
        scratch_shapes=[
            pltpu.VMEM(queries.shape, bf16),
            pltpu.VMEM((2,) + keys.shape, bf16),
            pltpu.VMEM((members, rows, heads * HD), bf16),
            pltpu.VMEM((2, seq_size * rows, HD), bf16),
            pltpu.VMEM(out_weight.shape, bf16),
            pltpu.VMEM((members * rows, tile_mask.shape[0]), bf16),
            pltpu.VMEM((heads, members, rows, 1), f32),
            pltpu.VMEM((heads, members, rows, 2 * HD), f32),
            pltpu.VMEM((members, rows, heads * HD), bf16),
            pltpu.VMEM((members, rows, heads * HD), bf16),
            pltpu.VMEM((blocks, rows, width), f32),
            pltpu.VMEM((blocks, rows, width), bf16),
            pltpu.VMEM((blocks, rows // cores, width), bf16),
            DMA((3,)),
            DMA,
            DMA((planes, local_groups, 2)),
            DMA((seq_size,)),
            DMA((local_groups, cores)),
            DMA((members,)),
            DMA((planes,)),
            DMA((planes,)),
            DMA((members,)),
            DMA((members,)),
            DMA((blocks,)),
            DMA((blocks,)),
        ],
        compiler_params=pltpu.CompilerParams(
            collective_id=0, has_side_effects=True, vmem_limit_bytes=60 * 1024 * 1024
        ),
        name="attend_project",
    )(queries, keys, values, tile_mask, out_weight)


def solution(mesh):
    placed = (P("seq", "head"), P("seq", "head"), P("seq", "head"), P(), P("head", None))
    sizes = (mesh.shape["seq"], mesh.shape["head"])
    return jax.shard_map(
        functools.partial(per_device, sizes),
        mesh=mesh,
        in_specs=placed,
        out_specs=P(("seq", "head"), None),
        check_vma=False,
    )
```

time: 148 us -> 37.1 us (0.25)
  the two profiles are of different devices: /device:TPU:25 before, /device:TPU:21 now
where the time goes in v1:
time: 37.1 us; the launch traced here: 36.9 us
  Pallas kernels  35 us (94%)
  local copies, waits for them, and re-layouts  1.87 us (5%)
    pallas_call x1, Pallas kernels, per_device(): pl.pallas_call(functools.partial(fused_kernel, dims), out_shape=jax.Shape...  35 us
    unnamed x1, local copies, waits for them, and re-layouts  1.87 us

profile of v1, /device:TPU:21, one launch (start us, length us, event | category | flops | bytes accessed | tf_op | source)
XLA Modules:
  0.0 36.9 jit_solution(8877501396288659255)
XLA Ops:
  0.0 35.0 %attend_project.1 = bf16[64,4096]{1,0:T(8,128)(2,1)} custom-call(bf16[128,1024]{1,0:T(8,128)(2,1)} %q_hbm.1, bf16[128,256]{1,0:T(8,128)(2,1)} %k_hbm.1, bf16[128,256]{1,0:T(8,128)(2,1)} %v_hbm.1, s32[32,32]{1,0:T(8,128)} %mask_ref.1, bf16[1024,4096]{1,0:T(8,128)(2,1)} %w_hbm.1), custom_call_target="tpu_custom_call" | custom-call | tf_op jit(solution)/shard_map/attend_project/pallas_call | solution.py:332
  35.0 1.9 %copy.7 = bf16[64,4096]{1,0:T(8,128)(2,1)} copy(bf16[64,4096]{1,0:T(8,128)(2,1)} %attend_project.1) | data formatting | bytes 1048576

commit v2 on v1

v2 whole, which is shorter than its diff:
```python
import functools
import math

import jax
import jax.numpy as jnp
from jax import lax
from jax.experimental import pallas as pl
from jax.experimental.pallas import tpu as pltpu
from jax.sharding import PartitionSpec as P

HD = 128
MASK_FLOOR = -1e30
MESH = pl.DeviceIdType.MESH


def fused_kernel(
    dims,
    q_hbm, k_hbm, v_hbm, mask_ref, w_hbm,
    out_ref,
    q_in, kv_in, qbuf, qext, kvbuf, spread, wbuf, best, acc, attbuf, abuf, part, sendbuf, rbuf,
    load_sem, w_sem, kv_send, kv_recv, q_send, q_recv, z_send, fwd_send, fwd_recv,
    a_send, a_recv, p_send, p_recv,
):
    planes, members, cores, local_groups, rows, heads, tile, blocks, width = dims
    place = lax.axis_index("seq")
    core = lax.axis_index("head")
    plane = place // members
    member = lax.rem(place, members)
    partner = 1 - core
    home = member // local_groups
    chunk = members * rows
    hw = heads * HD

    loads = [
        pltpu.make_async_copy(k_hbm, kv_in.at[0], load_sem.at[0]),
        pltpu.make_async_copy(v_hbm, kv_in.at[1], load_sem.at[1]),
        pltpu.make_async_copy(q_hbm, q_in, load_sem.at[2]),
    ]
    for load in loads:
        load.start()

    barrier = pltpu.get_barrier_semaphore()

    def greet(seq_to, head_to):
        pl.semaphore_signal(barrier, inc=1, device_id=(seq_to, head_to), device_id_type=MESH)

    for shift in range(1, members * cores):
        other = lax.rem(member * cores + core + shift, members * cores)
        greet(plane * members + other // cores, lax.rem(other, cores))

    @pl.when(plane < planes - 1)
    def _():
        greet(place + members, core)

    @pl.when(plane > 0)
    def _():
        greet(place - members, core)

    w_copy = pltpu.make_async_copy(w_hbm, wbuf, w_sem)

    tiles = mask_ref.shape[0]
    wide = qext.shape[2] - HD
    row_at = plane * chunk + lax.broadcasted_iota(jnp.int32, (chunk, tiles), 0)
    tile_at = lax.broadcasted_iota(jnp.int32, (chunk, tiles), 1) * tile
    pick = jnp.where((row_at >= tile_at) & (row_at < tile_at + tile), 1.0, 0.0).astype(jnp.bfloat16)
    closed = jnp.where(mask_ref[...] > 0, 0.0, 1.0).astype(jnp.bfloat16)
    if wide > tiles:
        closed = jnp.concatenate([closed, jnp.zeros((tiles, wide - tiles), jnp.bfloat16)], axis=1)
    shut = jnp.dot(pick, closed, preferred_element_type=jnp.float32)
    floor = jnp.where(shut > 0.5, MASK_FLOOR, 0.0).astype(jnp.bfloat16)
    for s in range(members):
        for h in range(heads):
            qext[s, h * rows : (h + 1) * rows, HD:] = floor[s * rows : (s + 1) * rows, :]

    for load in loads:
        load.wait()
    pl.semaphore_wait(
        barrier,
        members * cores - 1 + jnp.minimum(plane, 1) + jnp.minimum(planes - 1 - plane, 1),
    )

    def is_own(l, kind):
        return (core * local_groups + l == member) & (core == kind)

    def block_at(index):
        return pl.ds(pl.multiple_of(index * rows, rows), rows)

    def kv_copy(l, kind):
        return pltpu.make_async_remote_copy(
            src_ref=kv_in.at[kind, :, pl.ds(l * HD, HD)],
            dst_ref=kvbuf.at[kind, block_at(place), :],
            send_sem=kv_send.at[l, kind],
            recv_sem=kv_recv.at[place],
            device_id=(plane * members + core * local_groups + l, kind),
            device_id_type=MESH,
        )

    for l in range(local_groups):
        for kind in range(2):

            @pl.when(is_own(l, kind))
            def _():
                pltpu.make_async_copy(
                    kv_in.at[kind, :, pl.ds(l * HD, HD)],
                    kvbuf.at[kind, block_at(place), :],
                    kv_recv.at[place],
                ).start()

            @pl.when(jnp.logical_not(is_own(l, kind)))
            def _():
                kv_copy(l, kind).start()

    def q_copy(l, e):
        return pltpu.make_async_remote_copy(
            src_ref=q_in.at[:, pl.ds((l * cores + e) * hw, hw)],
            dst_ref=qbuf.at[member],
            send_sem=q_send.at[l, e],
            recv_sem=q_recv.at[member],
            device_id=(plane * members + core * local_groups + l, e),
            device_id_type=MESH,
        )

    for l in range(local_groups):
        for e in range(cores):

            @pl.when(is_own(l, e))
            def _():
                pltpu.make_async_copy(
                    q_in.at[:, pl.ds((l * cores + e) * hw, hw)], qbuf.at[member], q_recv.at[member]
                ).start()

            @pl.when(jnp.logical_not(is_own(l, e)))
            def _():
                q_copy(l, e).start()

    w_copy.start()

    def z_copy(index):
        return pltpu.make_async_remote_copy(
            src_ref=kvbuf.at[core, block_at(index), :],
            dst_ref=kvbuf.at[core, block_at(index), :],
            send_sem=z_send.at[index],
            recv_sem=kv_recv.at[index],
            device_id=(place + members, core),
            device_id_type=MESH,
        )

    def fwd_copy(index):
        return pltpu.make_async_remote_copy(
            src_ref=kvbuf.at[core, block_at(index), :],
            dst_ref=kvbuf.at[core, block_at(index), :],
            send_sem=fwd_send.at[index],
            recv_sem=fwd_recv.at[index],
            device_id=(place, partner),
            device_id_type=MESH,
        )

    def relay(kc, turn):
        across = lax.rem(member // 2 + turn // 2, members // 2) * 2
        index = kc * members + across + lax.rem(lax.rem(member, 2) + turn % 2, 2)
        block = kvbuf.at[core, block_at(index), :]
        pltpu.make_async_copy(block, block, kv_recv.at[index]).wait()

        @pl.when(plane < planes - 1)
        def _():
            z_copy(index).start()

        fwd_copy(index).start()

    def settle(kc):
        for s in range(members):
            block = kvbuf.at[partner, block_at(kc * members + s), :]
            pltpu.make_async_copy(block, block, fwd_recv.at[kc * members + s]).wait()
        key_at = kc * chunk + lax.broadcasted_iota(jnp.int32, (chunk, wide), 0)
        tile_from = lax.broadcasted_iota(jnp.int32, (chunk, wide), 1) * tile
        inside = (key_at >= tile_from) & (key_at < tile_from + tile)
        spread[...] = jnp.where(inside, 1.0, 0.0).astype(jnp.bfloat16)

    unit = math.log2(math.e) / math.sqrt(HD)

    def attend(kc, s, first):
        keys_here = (s + 1) * rows if first else chunk
        base = pl.multiple_of(kc * chunk, chunk)
        k_wide = jnp.concatenate([kvbuf[0, pl.ds(base, keys_here), :], spread[:keys_here, :]], axis=1)
        v_part = kvbuf[1, pl.ds(base, keys_here), :]
        v_wide = jnp.concatenate([v_part, jnp.ones_like(v_part)], axis=1)
        scores = lax.dot_general(
            qext[s], k_wide, (((1,), (1,)), ((), ())), preferred_element_type=jnp.float32
        )
        if first:
            r = s * rows + lax.broadcasted_iota(jnp.int32, (rows, keys_here), 0)
            u = lax.broadcasted_iota(jnp.int32, (rows, keys_here), 1)
            later = jnp.where(u <= r, 0.0, MASK_FLOOR)
            scores = scores + jnp.concatenate([later] * heads, axis=0)
        top = jnp.max(scores, axis=1, keepdims=True)
        if not first:
            before = best[s]
            top = jnp.maximum(before, top)
        weights = jnp.exp2((scores - top) * unit).astype(jnp.bfloat16)
        product = jnp.dot(weights, v_wide, preferred_element_type=jnp.float32)
        if not first:
            product = acc[s] * jnp.exp2((before - top) * unit) + product
        best[s] = top
        acc[s] = product

    slot = lax.rem(member, local_groups) * cores + core

    def a_copy(s):
        return pltpu.make_async_remote_copy(
            src_ref=attbuf.at[s],
            dst_ref=abuf.at[slot],
            send_sem=a_send.at[s],
            recv_sem=a_recv.at[slot],
            device_id=(plane * members + s, home),
            device_id_type=MESH,
        )

    def a_is_own(s):
        return (member == s) & (core == home)

    def give_back(s):
        for h in range(heads):
            total = acc[s, h * rows : (h + 1) * rows, :]
            attbuf[s, :, h * HD : (h + 1) * HD] = (total[:, :HD] / total[:, HD:]).astype(jnp.bfloat16)

        @pl.when(a_is_own(s))
        def _():
            pltpu.make_async_copy(attbuf.at[s], abuf.at[slot], a_recv.at[slot]).start()

        @pl.when(jnp.logical_not(a_is_own(s)))
        def _():
            a_copy(s).start()

    for t in range(members):
        relay(plane, t)

    @pl.when(plane >= 1)
    def _():
        for t in range(members):
            relay(plane - 1, t)

    settle(plane)
    for s in range(members):

        @pl.when(plane >= 2)
        def _():
            relay(plane - 2, s)

        block = qbuf.at[s]
        pltpu.make_async_copy(block, block, q_recv.at[s]).wait()
        for h in range(heads):
            qext[s, h * rows : (h + 1) * rows, :HD] = qbuf[s, :, h * HD : (h + 1) * HD]
        attend(plane, s, True)

    def below(step, none):
        settle(plane - step)
        for s in range(members):

            @pl.when(step + 2 <= plane)
            def _():
                relay(plane - step - 2, s)

            attend(plane - step, s, False)
        return none

    lax.fori_loop(1, plane, below, 0)

    @pl.when(plane >= 1)
    def _():
        settle(0)
        for s in range(members):
            attend(0, s, False)
            give_back(s)

    @pl.when(plane == 0)
    def _():
        for s in range(members):
            give_back(s)

    w_copy.wait()
    for j in range(local_groups * cores):
        block = abuf.at[j]
        pltpu.make_async_copy(block, block, a_recv.at[j]).wait()

    half = rows // cores
    attended = jnp.concatenate([abuf[j] for j in range(local_groups * cores)], axis=1)

    def p_copy(j):
        return pltpu.make_async_remote_copy(
            src_ref=sendbuf.at[j, pl.ds(pl.multiple_of(partner * half, half), half), :],
            dst_ref=rbuf.at[j],
            send_sem=p_send.at[j],
            recv_sem=p_recv.at[j],
            device_id=(place, partner),
            device_id_type=MESH,
        )

    for j in range(blocks):
        product = jnp.dot(
            attended, wbuf[:, j * width : (j + 1) * width], preferred_element_type=jnp.float32
        )
        sendbuf[j] = product.astype(jnp.bfloat16)
        p_copy(j).start()
        part[j] = product
    for j in range(blocks):
        p_copy(j).wait_recv()
        mine = part[j, pl.ds(pl.multiple_of(core * half, half), half), :]
        out_ref[:, j * width : (j + 1) * width] = (mine + rbuf[j].astype(jnp.float32)).astype(
            out_ref.dtype
        )

    for j in range(blocks):
        p_copy(j).wait_send()
    for s in range(members):

        @pl.when(jnp.logical_not(a_is_own(s)))
        def _():
            a_copy(s).wait_send()

    for l in range(local_groups):
        for e in range(cores):

            @pl.when(jnp.logical_not(is_own(l, e)))
            def _():
                q_copy(l, e).wait_send()
                kv_copy(l, e).wait_send()

    def drain(index, none):
        fwd_copy(index).wait_send()

        @pl.when(plane < planes - 1)
        def _():
            z_copy(index).wait_send()

        return none

    lax.fori_loop(0, (plane + 1) * members, drain, 0)


def per_device(sizes, queries, keys, values, tile_mask, out_weight):
    seq_size, cores = sizes
    rows = queries.shape[0]
    local_groups = keys.shape[1] // HD
    group = queries.shape[1] // HD // local_groups
    members = local_groups * cores
    planes = seq_size // members
    heads = group // cores
    tile = rows * seq_size // tile_mask.shape[0]
    columns = out_weight.shape[1]
    wide = -(-tile_mask.shape[0] // HD) * HD
    width = math.gcd(columns, 512)
    blocks = columns // width
    dims = (planes, members, cores, local_groups, rows, heads, tile, blocks, width)
    bf16, f32 = jnp.bfloat16, jnp.float32
    DMA = pltpu.SemaphoreType.DMA
    any_spec = pl.BlockSpec(memory_space=pl.ANY)
    vmem_spec = pl.BlockSpec(memory_space=pltpu.VMEM)
    return pl.pallas_call(
        functools.partial(fused_kernel, dims),
        out_shape=jax.ShapeDtypeStruct((rows // cores, columns), bf16),
        in_specs=[any_spec, any_spec, any_spec, vmem_spec, any_spec],
        out_specs=vmem_spec,
        scratch_shapes=[
            pltpu.VMEM(queries.shape, bf16),
            pltpu.VMEM((2,) + keys.shape, bf16),
            pltpu.VMEM((members, rows, heads * HD), bf16),
            pltpu.VMEM((members, heads * rows, HD + wide), bf16),
            pltpu.VMEM((2, seq_size * rows, HD), bf16),
            pltpu.VMEM((members * rows, wide), bf16),
            pltpu.VMEM(out_weight.shape, bf16),
            pltpu.VMEM((members, heads * rows, 1), f32),
            pltpu.VMEM((members, heads * rows, 2 * HD), f32),
            pltpu.VMEM((members, rows, heads * HD), bf16),
            pltpu.VMEM((members, rows, heads * HD), bf16),
            pltpu.VMEM((blocks, rows, width), f32),
            pltpu.VMEM((blocks, rows, width), bf16),
            pltpu.VMEM((blocks, rows // cores, width), bf16),
            DMA((3,)),
            DMA,
            DMA((local_groups, 2)),
            DMA((seq_size,)),
            DMA((local_groups, cores)),
            DMA((members,)),
            DMA((seq_size,)),
            DMA((seq_size,)),
            DMA((seq_size,)),
            DMA((members,)),
            DMA((members,)),
            DMA((blocks,)),
            DMA((blocks,)),
        ],
        compiler_params=pltpu.CompilerParams(
            collective_id=0, has_side_effects=True, vmem_limit_bytes=60 * 1024 * 1024
        ),
        name="attend_project",
    )(queries, keys, values, tile_mask, out_weight)


def solution(mesh):
    placed = (P("seq", "head"), P("seq", "head"), P("seq", "head"), P(), P("head", None))
    sizes = (mesh.shape["seq"], mesh.shape["head"])
    return jax.shard_map(
        functools.partial(per_device, sizes),
        mesh=mesh,
        in_specs=placed,
        out_specs=P(("seq", "head"), None),
        check_vma=False,
    )
```

time: 37.1 us -> 34.3 us (0.925)
  the two profiles are of different devices: /device:TPU:21 before, /device:TPU:31 now
where the time goes in v2:
time: 34.3 us; the launch traced here: 34.1 us
  Pallas kernels  32.2 us (94%)
  local copies, waits for them, and re-layouts  1.87 us (5%)
    pallas_call x1, Pallas kernels, per_device(): pl.pallas_call(functools.partial(fused_kernel, dims), out_shape=jax.Shape...  32.2 us
    unnamed x1, local copies, waits for them, and re-layouts  1.87 us

profile of v2, /device:TPU:31, one launch (start us, length us, event | category | flops | bytes accessed | tf_op | source)
XLA Modules:
  0.0 34.1 jit_solution(13258754584624833529)
XLA Ops:
  0.0 32.2 %attend_project.1 = bf16[64,4096]{1,0:T(8,128)(2,1)} custom-call(bf16[128,1024]{1,0:T(8,128)(2,1)} %q_hbm.1, bf16[128,256]{1,0:T(8,128)(2,1)} %k_hbm.1, bf16[128,256]{1,0:T(8,128)(2,1)} %v_hbm.1, s32[32,32]{1,0:T(8,128)} %mask_ref.1, bf16[1024,4096]{1,0:T(8,128)(2,1)} %w_hbm.1), custom_call_target="tpu_custom_call" | custom-call | tf_op jit(solution)/shard_map/attend_project/pallas_call | solution.py:358
  32.2 1.9 %copy.7 = bf16[64,4096]{1,0:T(8,128)(2,1)} copy(bf16[64,4096]{1,0:T(8,128)(2,1)} %attend_project.1) | data formatting | bytes 1048576

commit v3 on v2

v3 whole, which is shorter than its diff:
```python
import functools
import math

import jax
import jax.numpy as jnp
from jax import lax
from jax.experimental import pallas as pl
from jax.experimental.pallas import tpu as pltpu
from jax.sharding import PartitionSpec as P

HD = 128
MASK_FLOOR = -1e30
MESH = pl.DeviceIdType.MESH


def fused_kernel(
    dims,
    q_hbm, k_hbm, v_hbm, mask_hbm, w_hbm,
    out_ref,
    mask_ref, q_in, kv_in, qbuf, qext, kvbuf, spread, wbuf, best, acc, attbuf, abuf, part, sendbuf, rbuf,
    load_sem, w_sem, kv_send, kv_recv, q_send, q_recv, z_send, fwd_send, fwd_recv,
    a_send, a_recv, p_send, p_recv,
):
    planes, members, cores, local_groups, rows, heads, tile, blocks, width = dims
    place = lax.axis_index("seq")
    core = lax.axis_index("head")
    plane = place // members
    member = lax.rem(place, members)
    partner = 1 - core
    home = member // local_groups
    chunk = members * rows
    hw = heads * HD

    loads = [
        pltpu.make_async_copy(k_hbm, kv_in.at[0], load_sem.at[0]),
        pltpu.make_async_copy(v_hbm, kv_in.at[1], load_sem.at[1]),
        pltpu.make_async_copy(q_hbm, q_in, load_sem.at[2]),
        pltpu.make_async_copy(mask_hbm, mask_ref, load_sem.at[3]),
    ]
    for load in loads:
        load.start()

    barrier = pltpu.get_barrier_semaphore()

    def greet(seq_to, head_to):
        pl.semaphore_signal(barrier, inc=1, device_id=(seq_to, head_to), device_id_type=MESH)

    for shift in range(1, members * cores):
        peer = lax.rem(member * cores + core + shift, members * cores)
        greet(plane * members + peer // cores, lax.rem(peer, cores))

    @pl.when(plane < planes - 1)
    def _():
        greet(place + members, core)

    @pl.when(plane > 0)
    def _():
        greet(place - members, core)

    w_copy = pltpu.make_async_copy(w_hbm, wbuf, w_sem)

    for load in loads[:2]:
        load.wait()
    pl.semaphore_wait(
        barrier,
        members * cores - 1 + jnp.minimum(plane, 1) + jnp.minimum(planes - 1 - plane, 1),
    )

    def is_own(l, kind):
        return (core * local_groups + l == member) & (core == kind)

    def block_at(index):
        return pl.ds(pl.multiple_of(index * rows, rows), rows)

    def kv_copy(l, kind):
        return pltpu.make_async_remote_copy(
            src_ref=kv_in.at[kind, :, pl.ds(l * HD, HD)],
            dst_ref=kvbuf.at[kind, block_at(place), :],
            send_sem=kv_send.at[l, kind],
            recv_sem=kv_recv.at[place],
            device_id=(plane * members + core * local_groups + l, kind),
            device_id_type=MESH,
        )

    for l in range(local_groups):
        for kind in range(2):

            @pl.when(is_own(l, kind))
            def _():
                pltpu.make_async_copy(
                    kv_in.at[kind, :, pl.ds(l * HD, HD)],
                    kvbuf.at[kind, block_at(place), :],
                    kv_recv.at[place],
                ).start()

            @pl.when(jnp.logical_not(is_own(l, kind)))
            def _():
                kv_copy(l, kind).start()

    for load in loads[2:]:
        load.wait()

    def q_copy(l, e):
        return pltpu.make_async_remote_copy(
            src_ref=q_in.at[:, pl.ds((l * cores + e) * hw, hw)],
            dst_ref=qbuf.at[member],
            send_sem=q_send.at[l, e],
            recv_sem=q_recv.at[member],
            device_id=(plane * members + core * local_groups + l, e),
            device_id_type=MESH,
        )

    for l in range(local_groups):
        for e in range(cores):

            @pl.when(is_own(l, e))
            def _():
                pltpu.make_async_copy(
                    q_in.at[:, pl.ds((l * cores + e) * hw, hw)], qbuf.at[member], q_recv.at[member]
                ).start()

            @pl.when(jnp.logical_not(is_own(l, e)))
            def _():
                q_copy(l, e).start()

    w_copy.start()

    def z_copy(index):
        return pltpu.make_async_remote_copy(
            src_ref=kvbuf.at[core, block_at(index), :],
            dst_ref=kvbuf.at[core, block_at(index), :],
            send_sem=z_send.at[index],
            recv_sem=kv_recv.at[index],
            device_id=(place + members, core),
            device_id_type=MESH,
        )

    def fwd_copy(index):
        return pltpu.make_async_remote_copy(
            src_ref=kvbuf.at[core, block_at(index), :],
            dst_ref=kvbuf.at[core, block_at(index), :],
            send_sem=fwd_send.at[index],
            recv_sem=fwd_recv.at[index],
            device_id=(place, partner),
            device_id_type=MESH,
        )

    def other(turn):
        across = lax.rem(member // 2 + turn // 2, members // 2) * 2
        return across + lax.rem(lax.rem(member, 2) + turn % 2, 2)

    def relay(kc, turn):
        index = kc * members + other(turn)
        block = kvbuf.at[core, block_at(index), :]
        pltpu.make_async_copy(block, block, kv_recv.at[index]).wait()

        @pl.when(plane < planes - 1)
        def _():
            z_copy(index).start()

        fwd_copy(index).start()

    def settle(kc):
        for s in range(members):
            block = kvbuf.at[partner, block_at(kc * members + s), :]
            pltpu.make_async_copy(block, block, fwd_recv.at[kc * members + s]).wait()
        key_at = kc * chunk + lax.broadcasted_iota(jnp.int32, (chunk, wide), 0)
        tile_from = lax.broadcasted_iota(jnp.int32, (chunk, wide), 1) * tile
        inside = (key_at >= tile_from) & (key_at < tile_from + tile)
        spread[...] = jnp.where(inside, 1.0, 0.0).astype(jnp.bfloat16)

    unit = math.log2(math.e) / math.sqrt(HD)

    def attend(kc, parts, first):
        base = pl.multiple_of(kc * chunk, chunk)
        olds = [None if first else (best[s], acc[s]) for s in parts]
        news = []
        for s, old in zip(parts, olds):
            keys_here = (s + 1) * rows if first else chunk
            k_part = kvbuf[0, pl.ds(base, keys_here), :]
            k_wide = jnp.concatenate([k_part, spread[:keys_here, :]], axis=1)
            v_part = kvbuf[1, pl.ds(base, keys_here), :]
            v_wide = jnp.concatenate([v_part, jnp.ones_like(v_part)], axis=1)
            scores = lax.dot_general(
                qext[s], k_wide, (((1,), (1,)), ((), ())), preferred_element_type=jnp.float32
            )
            if first:
                r = s * rows + lax.broadcasted_iota(jnp.int32, (rows, keys_here), 0)
                u = lax.broadcasted_iota(jnp.int32, (rows, keys_here), 1)
                later = jnp.where(u <= r, 0.0, MASK_FLOOR)
                scores = scores + jnp.concatenate([later] * heads, axis=0)
            top = jnp.max(scores, axis=1, keepdims=True)
            if not first:
                top = jnp.maximum(old[0], top)
            weights = jnp.exp2((scores - top) * unit).astype(jnp.bfloat16)
            product = jnp.dot(weights, v_wide, preferred_element_type=jnp.float32)
            if not first:
                product = old[1] * jnp.exp2((old[0] - top) * unit) + product
            news.append((top, product))
        for s, new in zip(parts, news):
            best[s] = new[0]
            acc[s] = new[1]
        return news

    slot = lax.rem(member, local_groups) * cores + core

    def a_copy(s):
        return pltpu.make_async_remote_copy(
            src_ref=attbuf.at[s],
            dst_ref=abuf.at[slot],
            send_sem=a_send.at[s],
            recv_sem=a_recv.at[slot],
            device_id=(plane * members + s, home),
            device_id_type=MESH,
        )

    def a_is_own(s):
        return (member == s) & (core == home)

    def give_back(s, total):
        for h in range(heads):
            mine = total[h * rows : (h + 1) * rows, :]
            attbuf[s, :, h * HD : (h + 1) * HD] = (mine[:, :HD] / mine[:, HD:]).astype(jnp.bfloat16)

        @pl.when(a_is_own(s))
        def _():
            pltpu.make_async_copy(attbuf.at[s], abuf.at[slot], a_recv.at[slot]).start()

        @pl.when(jnp.logical_not(a_is_own(s)))
        def _():
            a_copy(s).start()

    for t in range(members):
        relay(plane, t)

    @pl.when(plane >= 1)
    def _():
        for t in range(members):
            relay(plane - 1, t)

    tiles = mask_ref.shape[0]
    wide = qext.shape[2] - HD
    row_at = plane * chunk + lax.broadcasted_iota(jnp.int32, (chunk, tiles), 0)
    tile_at = lax.broadcasted_iota(jnp.int32, (chunk, tiles), 1) * tile
    pick = jnp.where((row_at >= tile_at) & (row_at < tile_at + tile), 1.0, 0.0).astype(jnp.bfloat16)
    closed = jnp.where(mask_ref[...] > 0, 0.0, 1.0).astype(jnp.bfloat16)
    if wide > tiles:
        closed = jnp.concatenate([closed, jnp.zeros((tiles, wide - tiles), jnp.bfloat16)], axis=1)
    shut = jnp.dot(pick, closed, preferred_element_type=jnp.float32)
    floor = jnp.where(shut > 0.5, MASK_FLOOR, 0.0).astype(jnp.bfloat16)
    for s in range(members):
        for h in range(heads):
            qext[s, h * rows : (h + 1) * rows, HD:] = floor[s * rows : (s + 1) * rows, :]

    settle(plane)
    for pair in range(0, members, 2):

        @pl.when(plane >= 2)
        def _():
            relay(plane - 2, pair)
            relay(plane - 2, pair + 1)

        for s in (pair, pair + 1):
            block = qbuf.at[s]
            pltpu.make_async_copy(block, block, q_recv.at[s]).wait()
            for h in range(heads):
                qext[s, h * rows : (h + 1) * rows, :HD] = qbuf[s, :, h * HD : (h + 1) * HD]
        attend(plane, (pair, pair + 1), True)

    def below(step, none):
        settle(plane - step)
        for pair in range(0, members, 2):

            @pl.when(step + 2 <= plane)
            def _():
                relay(plane - step - 2, pair)
                relay(plane - step - 2, pair + 1)

            attend(plane - step, (pair, pair + 1), False)
        return none

    lax.fori_loop(1, plane, below, 0)

    @pl.when(plane >= 1)
    def _():
        settle(0)
        for pair in range(members // 2 - 1, -1, -1):
            parts = (other(2 * pair + 1), other(2 * pair))
            news = attend(0, parts, False)
            for s, new in zip(parts, news):
                give_back(s, new[1])

    @pl.when(plane == 0)
    def _():
        for turn in range(members - 1, -1, -1):
            s = other(turn)
            give_back(s, acc[s])

    w_copy.wait()
    for j in range(local_groups * cores):
        block = abuf.at[j]
        pltpu.make_async_copy(block, block, a_recv.at[j]).wait()

    half = rows // cores
    attended = jnp.concatenate([abuf[j] for j in range(local_groups * cores)], axis=1)

    def p_copy(j):
        return pltpu.make_async_remote_copy(
            src_ref=sendbuf.at[j, pl.ds(pl.multiple_of(partner * half, half), half), :],
            dst_ref=rbuf.at[j],
            send_sem=p_send.at[j],
            recv_sem=p_recv.at[j],
            device_id=(place, partner),
            device_id_type=MESH,
        )

    for j in range(blocks):
        product = jnp.dot(
            attended, wbuf[:, j * width : (j + 1) * width], preferred_element_type=jnp.float32
        )
        sendbuf[j] = product.astype(jnp.bfloat16)
        p_copy(j).start()
        part[j] = product
    for j in range(blocks):
        p_copy(j).wait_recv()
        mine = part[j, pl.ds(pl.multiple_of(core * half, half), half), :]
        out_ref[:, j * width : (j + 1) * width] = (mine + rbuf[j].astype(jnp.float32)).astype(
            out_ref.dtype
        )

    for j in range(blocks):
        p_copy(j).wait_send()
    for s in range(members):

        @pl.when(jnp.logical_not(a_is_own(s)))
        def _():
            a_copy(s).wait_send()

    for l in range(local_groups):
        for e in range(cores):

            @pl.when(jnp.logical_not(is_own(l, e)))
            def _():
                q_copy(l, e).wait_send()
                kv_copy(l, e).wait_send()

    def drain(index, none):
        fwd_copy(index).wait_send()

        @pl.when(plane < planes - 1)
        def _():
            z_copy(index).wait_send()

        return none

    lax.fori_loop(0, (plane + 1) * members, drain, 0)


def per_device(sizes, queries, keys, values, tile_mask, out_weight):
    seq_size, cores = sizes
    rows = queries.shape[0]
    local_groups = keys.shape[1] // HD
    group = queries.shape[1] // HD // local_groups
    members = local_groups * cores
    planes = seq_size // members
    heads = group // cores
    tile = rows * seq_size // tile_mask.shape[0]
    columns = out_weight.shape[1]
    wide = -(-tile_mask.shape[0] // HD) * HD
    width = math.gcd(columns, 512)
    blocks = columns // width
    dims = (planes, members, cores, local_groups, rows, heads, tile, blocks, width)
    bf16, f32 = jnp.bfloat16, jnp.float32
    DMA = pltpu.SemaphoreType.DMA
    any_spec = pl.BlockSpec(memory_space=pltpu.HBM)
    vmem_spec = pl.BlockSpec(memory_space=pltpu.VMEM)
    return pl.pallas_call(
        functools.partial(fused_kernel, dims),
        out_shape=jax.ShapeDtypeStruct((rows // cores, columns), bf16),
        in_specs=[any_spec] * 5,
        out_specs=vmem_spec,
        scratch_shapes=[
            pltpu.VMEM(tile_mask.shape, jnp.int32),
            pltpu.VMEM(queries.shape, bf16),
            pltpu.VMEM((2,) + keys.shape, bf16),
            pltpu.VMEM((members, rows, heads * HD), bf16),
            pltpu.VMEM((members, heads * rows, HD + wide), bf16),
            pltpu.VMEM((2, seq_size * rows, HD), bf16),
            pltpu.VMEM((members * rows, wide), bf16),
            pltpu.VMEM(out_weight.shape, bf16),
            pltpu.VMEM((members, heads * rows, 1), f32),
            pltpu.VMEM((members, heads * rows, 2 * HD), f32),
            pltpu.VMEM((members, rows, heads * HD), bf16),
            pltpu.VMEM((members, rows, heads * HD), bf16),
            pltpu.VMEM((blocks, rows, width), f32),
            pltpu.VMEM((blocks, rows, width), bf16),
            pltpu.VMEM((blocks, rows // cores, width), bf16),
            DMA((4,)),
            DMA,
            DMA((local_groups, 2)),
            DMA((seq_size,)),
            DMA((local_groups, cores)),
            DMA((members,)),
            DMA((seq_size,)),
            DMA((seq_size,)),
            DMA((seq_size,)),
            DMA((members,)),
            DMA((members,)),
            DMA((blocks,)),
            DMA((blocks,)),
        ],
        compiler_params=pltpu.CompilerParams(
            collective_id=0, has_side_effects=True, vmem_limit_bytes=60 << 20
        ),
        name="attend_project",
    )(queries, keys, values, tile_mask, out_weight)


def solution(mesh):
    placed = (P("seq", "head"), P("seq", "head"), P("seq", "head"), P(), P("head", None))
    sizes = (mesh.shape["seq"], mesh.shape["head"])
    return jax.shard_map(
        functools.partial(per_device, sizes),
        mesh=mesh,
        in_specs=placed,
        out_specs=P(("seq", "head"), None),
        check_vma=False,
    )
```

time: 34.3 us -> 31.8 us (0.927)
  the two profiles are of different devices: /device:TPU:31 before, /device:TPU:25 now
where the time goes in v3:
time: 31.8 us; the launch traced here: 31.6 us
  Pallas kernels  29.8 us (94%)
  local copies, waits for them, and re-layouts  1.87 us (6%)
    pallas_call x1, Pallas kernels, per_device(): pl.pallas_call(functools.partial(fused_kernel, dims), out_shape=jax.Shape...  29.8 us
    unnamed x1, local copies, waits for them, and re-layouts  1.87 us

profile of v3, /device:TPU:25, one launch (start us, length us, event | category | flops | bytes accessed | tf_op | source)
XLA Modules:
  0.0 31.6 jit_solution(14619664637329331157)
XLA Ops:
  0.0 29.8 %attend_project.1 = bf16[64,4096]{1,0:T(8,128)(2,1)} custom-call(bf16[128,1024]{1,0:T(8,128)(2,1)} %q_hbm.1, bf16[128,256]{1,0:T(8,128)(2,1)} %k_hbm.1, bf16[128,256]{1,0:T(8,128)(2,1)} %v_hbm.1, s32[32,32]{1,0:T(8,128)} %mask_hbm.1, bf16[1024,4096]{1,0:T(8,128)(2,1)} %w_hbm.1), custom_call_target="tpu_custom_call" | custom-call | tf_op jit(solution)/shard_map/attend_project/pallas_call | solution.py:377
  29.8 1.9 %copy.7 = bf16[64,4096]{1,0:T(8,128)(2,1)} copy(bf16[64,4096]{1,0:T(8,128)(2,1)} %attend_project.1) | data formatting | bytes 1048576

commit v4 on v3

--- a/solution.py
+++ b/solution.py
@@ -252,10 +252,11 @@
         for h in range(heads):
             qext[s, h * rows : (h + 1) * rows, HD:] = floor[s * rows : (s + 1) * rows, :]
 
+    ahead = jnp.where(plane < planes - 1, 2, 1)
     settle(plane)
     for pair in range(0, members, 2):
 
-        @pl.when(plane >= 2)
+        @pl.when((plane >= 2) & (plane < planes - 1))
         def _():
             relay(plane - 2, pair)
             relay(plane - 2, pair + 1)
@@ -271,10 +272,10 @@
         settle(plane - step)
         for pair in range(0, members, 2):
 
-            @pl.when(step + 2 <= plane)
-            def _():
-                relay(plane - step - 2, pair)
-                relay(plane - step - 2, pair + 1)
+            @pl.when(step + ahead <= plane)
+            def _():
+                relay(plane - step - ahead, pair)
+                relay(plane - step - ahead, pair + 1)
 
             attend(plane - step, (pair, pair + 1), False)
         return none
@@ -297,13 +298,7 @@
             give_back(s, acc[s])
 
     w_copy.wait()
-    for j in range(local_groups * cores):
-        block = abuf.at[j]
-        pltpu.make_async_copy(block, block, a_recv.at[j]).wait()
-
     half = rows // cores
-    attended = jnp.concatenate([abuf[j] for j in range(local_groups * cores)], axis=1)
-
     def p_copy(j):
         return pltpu.make_async_remote_copy(
             src_ref=sendbuf.at[j, pl.ds(pl.multiple_of(partner * half, half), half), :],
@@ -314,13 +309,24 @@
             device_id_type=MESH,
         )
 
-    for j in range(blocks):
-        product = jnp.dot(
-            attended, wbuf[:, j * width : (j + 1) * width], preferred_element_type=jnp.float32
-        )
-        sendbuf[j] = product.astype(jnp.bfloat16)
-        p_copy(j).start()
-        part[j] = product
+    for l in range(local_groups):
+        for e in range(cores):
+            block = abuf.at[l * cores + e]
+            pltpu.make_async_copy(block, block, a_recv.at[l * cores + e]).wait()
+        attended = jnp.concatenate([abuf[l * cores + e] for e in range(cores)], axis=1)
+        depth = cores * hw
+        for j in range(blocks):
+            product = jnp.dot(
+                attended,
+                wbuf[l * depth : (l + 1) * depth, j * width : (j + 1) * width],
+                preferred_element_type=jnp.float32,
+            )
+            if l > 0:
+                product = part[j] + product
+            if l == local_groups - 1:
+                sendbuf[j] = product.astype(jnp.bfloat16)
+                p_copy(j).start()
+            part[j] = product
     for j in range(blocks):
         p_copy(j).wait_recv()
         mine = part[j, pl.ds(pl.multiple_of(core * half, half), half), :]
@@ -367,7 +373,7 @@
     tile = rows * seq_size // tile_mask.shape[0]
     columns = out_weight.shape[1]
     wide = -(-tile_mask.shape[0] // HD) * HD
-    width = math.gcd(columns, 512)
+    width = math.gcd(columns, 2048)
     blocks = columns // width
     dims = (planes, members, cores, local_groups, rows, heads, tile, blocks, width)
     bf16, f32 = jnp.bfloat16, jnp.float32

time: 31.8 us -> 28.7 us (0.903)
  Pallas kernels: 29.8 us -> 26.7 us
    pallas_call x1, Pallas kernels: 29.8 us -> 26.7 us  [per_device(): pl.pallas_call(functools.partial(fused_kernel, dims), out_shape=jax.Shape...]
where the time goes in v4:
time: 28.7 us; the launch traced here: 28.6 us
  Pallas kernels  26.7 us (93%)
  local copies, waits for them, and re-layouts  1.87 us (7%)
    pallas_call x1, Pallas kernels, per_device(): pl.pallas_call(functools.partial(fused_kernel, dims), out_shape=jax.Shape...  26.7 us
    unnamed x1, local copies, waits for them, and re-layouts  1.87 us

profile of v4, /device:TPU:25, one launch (start us, length us, event | category | flops | bytes accessed | tf_op | source)
XLA Modules:
  0.0 28.6 jit_solution(11945346521337448989)
XLA Ops:
  0.0 26.7 %attend_project.1 = bf16[64,4096]{1,0:T(8,128)(2,1)} custom-call(bf16[128,1024]{1,0:T(8,128)(2,1)} %q_hbm.1, bf16[128,256]{1,0:T(8,128)(2,1)} %k_hbm.1, bf16[128,256]{1,0:T(8,128)(2,1)} %v_hbm.1, s32[32,32]{1,0:T(8,128)} %mask_hbm.1, bf16[1024,4096]{1,0:T(8,128)(2,1)} %w_hbm.1), custom_call_target="tpu_custom_call" | custom-call | tf_op jit(solution)/shard_map/attend_project/pallas_call | solution.py:383
  26.7 1.9 %copy.7 = bf16[64,4096]{1,0:T(8,128)(2,1)} copy(bf16[64,4096]{1,0:T(8,128)(2,1)} %attend_project.1) | data formatting | bytes 1048576
